TPU v7x, 32 devices: a whole 2x2x4 slice. The times are simulated.
32 devices in a mesh: row: 8 (over z, y), col: 4 (over x, core).
Axes of the slice: x: 2, y: 2, z: 4, core: 2. Of those that a mesh axis runs over, the one named last changes fastest.
Arguments:
- field: float32 [512, 64, 8, 512], P('row', 'col'), may hold values from -6 to 6
- modes: int32 [3, 256], replicated, may hold values from 0 to 511, as said below
Outputs:
- spectrum: float32 [64, 512, 8, 512], P(None, 'col', None, 'row')
- localized: float32 [512, 512], replicated
Inputs may be any that keep to these rules, and one draw needn't show every extreme that they name: `modes`: row 0 holds kx in 0 to 255, row 1 ky in 0 to 511, row 2 kz in 0 to 63; triples may repeat.
All inputs are finite; a program needn't handle non-finite values.
Results may differ from a plain program's by a relative error of at most 0.00013.
Values sent between devices are 32-bit elements; how exact they have to be, the bound alone decides.
A program may use at most 192 MiB of HBM per device.

v0:
```python
import math
import jax
import jax.numpy as jnp
from jax import lax
from jax.sharding import PartitionSpec as P

NX = 512
NY = 512
NZ = 64
REACH = 64
highest = lax.Precision.HIGHEST


def tables(length, count):
    points = lax.iota(jnp.int32, length)
    waves = lax.iota(jnp.int32, count)
    phase = points[:, None] * waves[None, :] % length
    angle = phase.astype(jnp.float32) * (2.0 * math.pi / length)
    return (jnp.cos(angle), jnp.sin(angle))


def rotation(count):
    source = lax.iota(jnp.int32, count)[:, None]
    target = lax.iota(jnp.int32, count)[None, :]
    even_out = target % 2 == 0
    plus = jnp.logical_and(source == target + 1, even_out).astype(jnp.float32)
    minus = jnp.logical_and(source + 1 == target, jnp.logical_not(even_out)).astype(jnp.float32)
    return plus - minus


def taper_of(modes, size_y, size_z, reach):
    first = modes[0].astype(jnp.float32)
    second = jnp.where(modes[1] < size_y // 2, modes[1], modes[1] - size_y).astype(jnp.float32)
    third = jnp.where(modes[2] < size_z // 2, modes[2], modes[2] - size_z).astype(jnp.float32)
    first = jnp.concatenate([first, first])
    second = jnp.concatenate([second, second])
    third = jnp.concatenate([third, third])
    dist = (first[:, None] - first[None, :]) ** 2 + (second[:, None] - second[None, :]) ** 2
    dist = dist + (third[:, None] - third[None, :]) ** 2
    return jnp.exp(-dist / (2.0 * reach * reach))


def y_transform(lines):
    length = lines.shape[0]
    cos_y, sin_y = tables(length, length)
    plain = jnp.einsum("ky,yzmq->kzmq", cos_y, lines, precision=highest)
    turned = jnp.einsum("ky,yzmq->kzmq", sin_y, lines, precision=highest)
    return plain + jnp.einsum("kzmq,qp->kzmp", turned, rotation(lines.shape[-1]), precision=highest)


def per_device(field, modes):
    members = field.shape[2]
    width = field.shape[3]
    cos_x, sin_x = tables(width, width // 2)
    x_table = jnp.stack([cos_x, -sin_x], axis=2).reshape(width, width)
    lines = jnp.einsum("yzmx,xq->yzmq", field, x_table, precision=highest)
    gathered = lax.all_to_all(lines, "row", split_axis=3, concat_axis=0, tiled=True)
    ytrans = y_transform(gathered)
    levels = lax.all_to_all(ytrans, "col", split_axis=0, concat_axis=1, tiled=True)
    depth = levels.shape[1]
    cos_z, sin_z = tables(depth, depth)
    plain = jnp.einsum("kz,yzmq->kymq", cos_z, levels, precision=highest)
    turned = jnp.einsum("kz,yzmq->kymq", sin_z, levels, precision=highest)
    combined = plain + jnp.einsum(
        "kymq,qp->kymp", turned, rotation(levels.shape[-1]), precision=highest
    )
    factor = 1.0 / math.sqrt(NX * NY * NZ)
    spectrum = combined * factor
    local_y = spectrum.shape[1]
    local_q = spectrum.shape[3]
    row_start = lax.axis_index("row") * local_q
    col_start = lax.axis_index("col") * local_y
    flat = spectrum.reshape(depth * local_y, members, local_q)
    offset = modes[1] - col_start
    inside_y = jnp.logical_and(offset >= 0, offset < local_y).astype(jnp.float32)
    index = modes[2] * local_y + jnp.clip(offset, 0, local_y - 1)
    picked_rows = flat[index]
    target = 2 * modes[0] - row_start
    columns = lax.iota(jnp.int32, local_q)[None, :]
    choose = jnp.stack([columns == target[:, None], columns == target[:, None] + 1], axis=2).astype(
        jnp.float32
    )
    choose = choose * inside_y[:, None, None]
    partial_value = jnp.einsum("smq,sqc->mcs", picked_rows, choose, precision=highest).reshape(
        members, -1
    )
    coef = lax.psum(partial_value, ("row", "col"))
    anomaly = coef - jnp.mean(coef, axis=0, keepdims=True)
    cov = jnp.dot(anomaly.T, anomaly, precision=highest) / (members - 1)
    localized = cov * taper_of(modes, NY, NZ, REACH)
    return (spectrum, localized)


def solution(mesh):
    placed = (P("row", "col", None, None), P())
    return jax.shard_map(
        per_device,
        mesh=mesh,
        in_specs=placed,
        out_specs=(P(None, "col", None, "row"), P()),
        check_vma=False,
    )
```

profile of v0, /device:TPU:0, one launch (start us, length us, event | category | flops | bytes accessed | tf_op | source)
XLA Modules:
  0.0 1293.4 jit_solution(5573586038033272029)
XLA Ops:
  4.6 40.4 %fusion.5 = f32[64,16,8,512]{3,0,2,1:T(8,128)} fusion(f32[64,16,8,512]{3,2,1,0:T(8,128)} %param.2, f32[512,512]{0,1:T(8,128)S(1)} %reshape.252), kind=kOutput, calls=%fused_computation.9 | convolution fusion | flops 25769803776 | bytes 34603008 | tf_op jit(solution)/shard_map/yzmx,xq->yzmq/dot_general | solution.py:56
  45.0 30.4 %copy.32 = f32[64,16,8,512]{0,2,1,3:T(8,128)} copy(f32[64,16,8,512]{3,0,2,1:T(8,128)} %fusion.5) | data formatting | bytes 33554432 | tf_op jit(solution)/shard_map/yzmx,xq->yzmq/dot_general | solution.py:56
  75.4 25.7 %reshape.273 = f32[8,1,524288]{2,1,0:T(1,128)} reshape(f32[512,16,8,64]{3,2,1,0:T(8,128)} %bitcast.65) | data formatting | bytes 33554432
  101.1 7.3 all-to-all-start
  108.4 363.1 %all-to-all-done = f32[8,1,524288]{2,1,0:T(1,128)} async-done(((f32[8,1,524288]{2,1,0:T(1,128)}), f32[8,1,524288]{2,1,0:T(1,128)}, u32[]{:S(2)}, u32[]{:S(2)}) %all-to-all-start) | async-done | bytes 16777248 | tf_op jit(solution)/shard_map/all_to_all | solution.py:57
  472.0 50.5 %reduce = f32[8,524288]{1,0:T(8,128)} reduce(f32[8,1,524288]{2,1,0:T(1,128)} %all-to-all-done, f32[]{:T(128)} %broadcast.368), dimensions={1}, to_apply=%all_to_all.26.reduce_sub_computation | reduce | bytes 33554436 | tf_op jit(solution)/shard_map/all_to_all | solution.py:57
  522.5 30.2 %reshape.274 = f32[512,16,8,64]{3,2,1,0:T(8,128)} reshape(f32[8,524288]{1,0:T(8,128)} %reduce) | data formatting | bytes 33554432
  552.7 31.9 %copy.60 = f32[64,16,8,8,64]{0,3,4,2,1:T(8,128)} copy(f32[64,16,8,8,64]{0,2,1,4,3:T(8,128)} %bitcast.67) | data formatting | bytes 33554432 | tf_op jit(solution)/shard_map/all_to_all | solution.py:57
  584.6 27.6 %reshape.264 = f32[512,8192]{0,1:T(8,128)} reshape(f32[8,64,16,8,64]{1,0,4,3,2:T(8,128)} %bitcast.68) | data formatting | bytes 33554432
  612.2 46.3 %fusion.15 = f32[512,8192]{0,1} fusion(f32[512,8192]{0,1:T(8,128)} %reshape.264), kind=kOutput, calls=%fused_computation.23 | convolution fusion | flops 25773473792 | bytes 33554432
  658.5 40.8 %fusion.13 = f32[512,8192]{0,1} fusion(f32[512,8192]{0,1:T(8,128)S(1)} %copy-done), kind=kOutput, calls=%fused_computation.21 | convolution fusion | flops 25773473792 | bytes 33554432
  699.3 22.7 %convolution_add_fusion = f32[512,16,8,64]{0,3,2,1:T(8,128)} fusion(f32[512,16,8,64]{0,3,2,1:T(8,128)} %bitcast.69, f32[512,16,8,64]{0,3,2,1:T(8,128)} %bitcast.70, s32[64]{0:T(128)S(1)} %iota_add_fusion, pred[64]{0:T(512)(128)(4,1)S(1)} %get-tuple-element.17, pred[64]{0:T(512)(128)(4,1)S(1)} %get-tuple-element.16), kind=kOutput, calls=%fused_computation.8 | convolution fusion | flops 3225448448 | bytes 50332032 | tf_op jit(solution)/shard_map/kzmq,qp->kzmp/dot_general | solution.py:48
  721.9 30.4 %copy.34 = f32[512,16,8,64]{3,2,1,0:T(8,128)} copy(f32[512,16,8,64]{0,3,2,1:T(8,128)} %convolution_add_fusion) | data formatting | bytes 33554432 | tf_op jit(solution)/shard_map/add | solution.py:48
  752.4 42.3 %reshape.275 = f32[4,1,1048576]{2,1,0:T(1,128)} reshape(f32[512,16,8,64]{3,2,1,0:T(8,128)} %copy.34) | data formatting | bytes 33554432
  802.1 182.7 %all-to-all-done.1 = f32[4,1,1048576]{2,1,0:T(1,128)} async-done(((f32[4,1,1048576]{2,1,0:T(1,128)}), f32[4,1,1048576]{2,1,0:T(1,128)}, u32[]{:S(2)}, u32[]{:S(2)}) %all-to-all-start.1) | async-done | bytes 16777248 | tf_op jit(solution)/shard_map/all_to_all | solution.py:59
  984.8 54.6 %reduce.1 = f32[4,1048576]{1,0:T(4,128)} reduce(f32[4,1,1048576]{2,1,0:T(1,128)} %all-to-all-done.1, f32[]{:T(128)} %broadcast.368), dimensions={1}, to_apply=%all_to_all.30.reduce_sub_computation | reduce | bytes 33554436 | tf_op jit(solution)/shard_map/all_to_all | solution.py:59
  1039.4 55.4 %reshape.276 = f32[512,16,8,64]{3,2,1,0:T(8,128)} reshape(f32[4,1048576]{1,0:T(4,128)} %reduce.1) | data formatting | bytes 33554432
  1094.8 24.7 %copy.35 = f32[4,128,16,8,64]{1,2,0,4,3:T(8,128)} copy(f32[4,128,16,8,64]{4,3,2,1,0:T(8,128)} %bitcast.66) | data formatting | bytes 33554432 | tf_op jit(solution)/shard_map/all_to_all | solution.py:59
  1119.5 21.7 %fusion.32 = f32[64,128,8,64]{1,0,3,2:T(8,128)} fusion(f32[128,64,8,64]{0,1,3,2:T(8,128)} %bitcast.63), kind=kOutput, calls=%fused_computation.48 | convolution fusion | flops 3221282816 | bytes 33554432 | tf_op jit(solution)/shard_map/kz,yzmq->kymq/dot_general | solution.py:63
  1141.2 36.6 %fusion.1 = f32[64,128,8,64]{1,3,2,0:T(8,128)} fusion(f32[64,128,8,64]{1,0,3,2:T(8,128)} %fusion.32, s32[64]{0:T(128)S(1)} %iota_add_fusion, pred[64]{0:T(512)(128)(4,1)S(1)} %get-tuple-element.17, pred[64]{0:T(512)(128)(4,1)S(1)} %get-tuple-element.16), kind=kOutput, calls=%fused_computation.4 | convolution fusion | flops 3221254144 | bytes 33554816 | tf_op jit(solution)/shard_map/kymq,qp->kymp/dot_general | solution.py:64
  1177.8 35.2 %fusion = f32[64,128,8,64]{1,0,3,2:T(8,128)} fusion(f32[64,128,8,64]{1,3,2,0:T(8,128)} %fusion.1, f32[128,64,8,64]{0,1,3,2:T(8,128)} %bitcast.64), kind=kOutput, calls=%fused_computation.3 | convolution fusion | flops 3229671424 | bytes 50331648 | tf_op jit(solution)/shard_map/kz,yzmq->kymq/dot_general | solution.py:62
  1213.0 20.0 %copy.47 = f32[64,128,8,64]{3,2,1,0:T(8,128)} copy(f32[64,128,8,64]{1,0,3,2:T(8,128)} %fusion) | data formatting | bytes 33554432 | tf_op jit(solution)/shard_map/reshape | solution.py:73
  1233.0 16.0 %copy.41 = f32[64,128,8,64]{1,3,2,0:T(8,128)} copy(f32[64,128,8,64]{1,0,3,2:T(8,128)} %fusion) | data formatting | bytes 33554432
  1253.3 37.6 %psum.7 = f32[8,512]{1,0:T(8,128)S(1)} all-reduce(f32[8,512]{1,0:T(8,128)S(1)} %bitcast.72), channel_id=1, replica_groups=mesh['row'=8,'col'=4] {'row','col'}, use_global_device_ids=true, to_apply=%region_0.1 | all-reduce | flops 4096 | bytes 32768 | tf_op jit(solution)/shard_map/psum | solution.py:87
  (30 shorter events, 18.4 us)
Async XLA Ops:
  101.1 370.4 %all-to-all-start = ((f32[8,1,524288]{2,1,0:T(1,128)}), f32[8,1,524288]{2,1,0:T(1,128)}, u32[]{:S(2)}, u32[]{:S(2)}) async-start(f32[8,1,524288]{2,1,0:T(1,128)} %reshape.273), calls=%async_computation | async-start | bytes 33554432 | tf_op jit(solution)/shard_map/all_to_all | solution.py:57
  612.2 46.3 %copy-start = (f32[512,8192]{0,1:T(8,128)S(1)}, f32[512,8192]{0,1:T(8,128)}, u32[]{:S(2)}) copy-start(f32[512,8192]{0,1:T(8,128)} %reshape.264) | copy-start | bytes 50331652
  794.6 7.1 copy-start.1
  794.6 190.1 %all-to-all-start.1 = ((f32[4,1,1048576]{2,1,0:T(1,128)}), f32[4,1,1048576]{2,1,0:T(1,128)}, u32[]{:S(2)}, u32[]{:S(2)}) async-start(f32[4,1,1048576]{2,1,0:T(1,128)} %reshape.275), calls=%async_computation.1 | async-start | bytes 33554432 | tf_op jit(solution)/shard_map/all_to_all | solution.py:59
where the time goes:
time: 1300 us; the launch traced here: 1290 us
  waiting for transfers between devices  546 us (42%)
  local copies, waits for them, and re-layouts  340 us (26%)
  matrix products  248 us (19%)
  other arithmetic  107 us (8%)
  blocking collectives  37.6 us (3%)
  starting transfers between devices  14.4 us (1%)
    all_to_all x1, waiting for transfers between devices, per_device(): lax.all_to_all(lines, 'row', split_axis=3, concat_axis=0, tiled=True)  363 us
    unnamed x11, local copies, waits for them, and re-layouts  197 us
    all_to_all x1, waiting for transfers between devices, per_device(): lax.all_to_all(ytrans, 'col', split_axis=0, concat_axis=1, tiled=True)  183 us
    unnamed x2, matrix products  87 us
    all_to_all x1, other arithmetic, per_device(): lax.all_to_all(ytrans, 'col', split_axis=0, concat_axis=1, tiled=True)  54.6 us
    all_to_all x1, other arithmetic, per_device(): lax.all_to_all(lines, 'row', split_axis=3, concat_axis=0, tiled=True)  50.5 us
    dot_general x1, matrix products, per_device(): lines = jnp.einsum('yzmx,xq->yzmq', field, x_table, precision=highest)  40.4 us
    psum x1, blocking collectives, per_device(): coef = lax.psum(partial_value, ('row', 'col'))  37.6 us
  transfers between devices with their start and end apart: 2, of which 2 were waited for; matrix products, arithmetic and copies ran while one was open for 0% of the time, Pallas kernels for 0%

commit v1 on v0

--- a/solution.py
+++ b/solution.py
@@ -1,3 +1,4 @@
+import functools
 import math
 import jax
 import jax.numpy as jnp
@@ -9,6 +10,17 @@
 NZ = 64
 REACH = 64
 highest = lax.Precision.HIGHEST
+
+
+def rounds_choose(z, axis_tag, at_axis, on_dim):
+    e_next = lax.axis_size(axis_tag)
+    wide_out = jnp.split(z, e_next, axis=at_axis)
+    left_arr = jnp.stack(wide_out, axis=0)
+    state_now = lax.all_to_all(left_arr, axis_tag, 0, 0)
+    return jnp.concatenate(state_now, axis=on_dim)
+
+
+_return_all_heads = functools.partial(rounds_choose, axis_tag="col", at_axis=0, on_dim=1)
 
 
 def tables(length, count):
@@ -56,7 +68,7 @@
     lines = jnp.einsum("yzmx,xq->yzmq", field, x_table, precision=highest)
     gathered = lax.all_to_all(lines, "row", split_axis=3, concat_axis=0, tiled=True)
     ytrans = y_transform(gathered)
-    levels = lax.all_to_all(ytrans, "col", split_axis=0, concat_axis=1, tiled=True)
+    levels = _return_all_heads(ytrans)
     depth = levels.shape[1]
     cos_z, sin_z = tables(depth, depth)
     plain = jnp.einsum("kz,yzmq->kymq", cos_z, levels, precision=highest)

time: 1300 us -> 1130 us (0.87)
  local copies, waits for them, and re-layouts: 340 us -> 193 us
  other arithmetic: 107 us -> 59 us
  matrix products: 248 us -> 270 us
    unnamed x11 -> x9, local copies, waits for them, and re-layouts: 197 us -> 99.6 us
    all_to_all x1 -> x0, other arithmetic: 54.6 us -> none  [per_device(): lax.all_to_all(ytrans, 'col', split_axis=0, concat_axis=1, tiled=True)]
    add x1 -> x0, local copies, waits for them, and re-layouts: 30.4 us -> none  [y_transform(): plain + jnp.einsum('kzmq,qp->kzmp', turned, rotation(lines.shape[-1]), pr...]
    all_to_all x1 -> x0, local copies, waits for them, and re-layouts: 24.7 us -> none  [per_device(): lax.all_to_all(ytrans, 'col', split_axis=0, concat_axis=1, tiled=True)]
where the time goes in v1:
time: 1130 us; the launch traced here: 1120 us
  waiting for transfers between devices  546 us (48%)
  matrix products  270 us (24%)
  local copies, waits for them, and re-layouts  193 us (17%)
  other arithmetic  59 us (5%)
  blocking collectives  37.7 us (3%)
  starting transfers between devices  14.4 us (1%)
    all_to_all x1, waiting for transfers between devices, per_device(): lax.all_to_all(lines, 'row', split_axis=3, concat_axis=0, tiled=True)  363 us
    all_to_all x1, waiting for transfers between devices, rounds_choose(): state_now = lax.all_to_all(left_arr, axis_tag, 0, 0)  183 us
    unnamed x9, local copies, waits for them, and re-layouts  99.6 us
    unnamed x2, matrix products  86.8 us
    all_to_all x1, other arithmetic, per_device(): lax.all_to_all(lines, 'row', split_axis=3, concat_axis=0, tiled=True)  50.5 us
    dot_general x1, matrix products, per_device(): plain = jnp.einsum('kz,yzmq->kymq', cos_z, levels, precision=highest)  46.7 us
    dot_general x1, matrix products, per_device(): lines = jnp.einsum('yzmx,xq->yzmq', field, x_table, precision=highest)  40.4 us
    psum x1, blocking collectives, per_device(): coef = lax.psum(partial_value, ('row', 'col'))  37.7 us
  transfers between devices with their start and end apart: 2, of which 2 were waited for; matrix products, arithmetic and copies ran while one was open for 0% of the time, Pallas kernels for 0%

profile of v1, /device:TPU:0, one launch (start us, length us, event | category | flops | bytes accessed | tf_op | source)
XLA Modules:
  0.0 1121.5 jit_solution(13963024268899041357)
XLA Ops:
  4.3 40.4 %fusion.11 = f32[64,16,8,512]{3,0,2,1:T(8,128)} fusion(f32[64,16,8,512]{3,2,1,0:T(8,128)} %param.2, f32[512,512]{0,1:T(8,128)S(1)} %reshape.258), kind=kOutput, calls=%fused_computation.14 | convolution fusion | flops 25769803776 | bytes 34603008 | tf_op jit(solution)/shard_map/yzmx,xq->yzmq/dot_general | solution.py:68
  44.6 30.4 %copy.32 = f32[64,16,8,512]{0,2,1,3:T(8,128)} copy(f32[64,16,8,512]{3,0,2,1:T(8,128)} %fusion.11) | data formatting | bytes 33554432 | tf_op jit(solution)/shard_map/yzmx,xq->yzmq/dot_general | solution.py:68
  75.1 25.9 %reshape.281 = f32[8,1,524288]{2,1,0:T(1,128)} reshape(f32[512,16,8,64]{3,2,1,0:T(8,128)} %bitcast.68) | data formatting | bytes 33554432
  101.0 7.3 all-to-all-start
  108.3 363.0 %all-to-all-done = f32[8,1,524288]{2,1,0:T(1,128)} async-done(((f32[8,1,524288]{2,1,0:T(1,128)}), f32[8,1,524288]{2,1,0:T(1,128)}, u32[]{:S(2)}, u32[]{:S(2)}) %all-to-all-start) | async-done | bytes 16777248 | tf_op jit(solution)/shard_map/all_to_all | solution.py:69
  471.8 50.5 %reduce = f32[8,524288]{1,0:T(8,128)} reduce(f32[8,1,524288]{2,1,0:T(1,128)} %all-to-all-done, f32[]{:T(128)} %broadcast.368), dimensions={1}, to_apply=%all_to_all.16.reduce_sub_computation | reduce | bytes 33554436 | tf_op jit(solution)/shard_map/all_to_all | solution.py:69
  522.3 30.0 %reshape.282 = f32[512,16,8,64]{3,2,1,0:T(8,128)} reshape(f32[8,524288]{1,0:T(8,128)} %reduce) | data formatting | bytes 33554432
  552.3 31.9 %copy.66 = f32[64,16,8,8,64]{0,3,4,2,1:T(8,128)} copy(f32[64,16,8,8,64]{0,2,1,4,3:T(8,128)} %bitcast.69) | data formatting | bytes 33554432 | tf_op jit(solution)/shard_map/all_to_all | solution.py:69
  584.2 27.6 %reshape.272 = f32[512,8192]{0,1:T(8,128)} reshape(f32[8,64,16,8,64]{1,0,4,3,2:T(8,128)} %bitcast.70) | data formatting | bytes 33554432
  611.8 46.2 %fusion.21 = f32[512,8192]{0,1} fusion(f32[512,8192]{0,1:T(8,128)} %reshape.272), kind=kOutput, calls=%fused_computation.32 | convolution fusion | flops 25773473792 | bytes 33554432
  658.1 40.6 %fusion.19 = f32[512,8192]{0,1} fusion(f32[512,8192]{0,1:T(8,128)S(1)} %copy-done), kind=kOutput, calls=%fused_computation.30 | convolution fusion | flops 25773473792 | bytes 33554432
  698.7 22.7 %convolution_add_fusion = f32[512,16,8,64]{0,3,2,1:T(8,128)} fusion(f32[512,16,8,64]{0,3,2,1:T(8,128)} %bitcast.71, f32[512,16,8,64]{0,3,2,1:T(8,128)} %bitcast.72, s32[64]{0:T(128)S(1)} %iota_add_fusion, pred[64]{0:T(512)(128)(4,1)S(1)} %get-tuple-element.21, pred[64]{0:T(512)(128)(4,1)S(1)} %get-tuple-element.20), kind=kOutput, calls=%fused_computation.13 | convolution fusion | flops 3225448448 | bytes 50332032 | tf_op jit(solution)/shard_map/kzmq,qp->kzmp/dot_general | solution.py:60
  721.4 6.8 slice_bitcast_fusion.3
  728.2 6.2 pad_maximum_fusion
  734.5 7.1 all-to-all-start.1
  742.0 182.7 %all-to-all-done.1 = f32[4,128,16,8,64]{1,4,3,2,0:T(8,128)} async-done(((f32[4,128,16,8,64]{1,4,3,2,0:T(8,128)}), f32[4,128,16,8,64]{1,4,3,2,0:T(8,128)}, u32[]{:S(2)}, u32[]{:S(2)}) %all-to-all-start.1) | async-done | bytes 16777248 | tf_op jit(solution)/shard_map/all_to_all | solution.py:19
  924.6 33.2 %fusion.5 = f32[64,128,8,64]{1,0,3,2:T(8,128)} fusion(f32[128,64,8,64]{0,3,2,1:T(8,128)} %bitcast.15), kind=kOutput, calls=%fused_computation.9 | convolution fusion | flops 3221282816 | bytes 33554432 | tf_op jit(solution)/shard_map/kz,yzmq->kymq/dot_general | solution.py:75
  957.9 36.4 %fusion.1 = f32[64,128,8,64]{1,3,2,0:T(8,128)} fusion(f32[64,128,8,64]{1,0,3,2:T(8,128)} %fusion.5, s32[64]{0:T(128)S(1)} %iota_add_fusion, pred[64]{0:T(512)(128)(4,1)S(1)} %get-tuple-element.21, pred[64]{0:T(512)(128)(4,1)S(1)} %get-tuple-element.20), kind=kOutput, calls=%fused_computation.5 | convolution fusion | flops 3221254144 | bytes 33554816 | tf_op jit(solution)/shard_map/kymq,qp->kymp/dot_general | solution.py:76
  994.3 46.7 %fusion = f32[64,128,8,64]{1,0,3,2:T(8,128)} fusion(f32[64,128,8,64]{1,3,2,0:T(8,128)} %fusion.1, f32[128,64,8,64]{0,3,2,1:T(8,128)} %bitcast.15), kind=kOutput, calls=%fused_computation.4 | convolution fusion | flops 3229671424 | bytes 50331648 | tf_op jit(solution)/shard_map/kz,yzmq->kymq/dot_general | solution.py:74
  1041.0 20.0 %copy.47 = f32[64,128,8,64]{3,2,1,0:T(8,128)} copy(f32[64,128,8,64]{1,0,3,2:T(8,128)} %fusion) | data formatting | bytes 33554432 | tf_op jit(solution)/shard_map/reshape | solution.py:85
  1061.0 16.0 %copy.41 = f32[64,128,8,64]{1,3,2,0:T(8,128)} copy(f32[64,128,8,64]{1,0,3,2:T(8,128)} %fusion) | data formatting | bytes 33554432
  1077.0 2.3 gather_fusion
  1081.3 37.7 %psum.7 = f32[8,512]{1,0:T(8,128)S(1)} all-reduce(f32[8,512]{1,0:T(8,128)S(1)} %bitcast.74), channel_id=1, replica_groups=mesh['row'=8,'col'=4] {'row','col'}, use_global_device_ids=true, to_apply=%region_0.1 | all-reduce | flops 4096 | bytes 32768 | tf_op jit(solution)/shard_map/psum | solution.py:99
  1119.0 2.3 fusion.14
  (27 shorter events, 6.3 us)
Async XLA Ops:
  101.0 370.3 %all-to-all-start = ((f32[8,1,524288]{2,1,0:T(1,128)}), f32[8,1,524288]{2,1,0:T(1,128)}, u32[]{:S(2)}, u32[]{:S(2)}) async-start(f32[8,1,524288]{2,1,0:T(1,128)} %reshape.281), calls=%async_computation | async-start | bytes 33554432 | tf_op jit(solution)/shard_map/all_to_all | solution.py:69
  611.8 46.2 %copy-start = (f32[512,8192]{0,1:T(8,128)S(1)}, f32[512,8192]{0,1:T(8,128)}, u32[]{:S(2)}) copy-start(f32[512,8192]{0,1:T(8,128)} %reshape.272) | copy-start | bytes 50331652
  734.5 7.1 copy-start.1
  734.5 190.1 %all-to-all-start.1 = ((f32[4,128,16,8,64]{1,4,3,2,0:T(8,128)}), f32[4,128,16,8,64]{1,4,3,2,0:T(8,128)}, u32[]{:S(2)}, u32[]{:S(2)}) async-start(f32[4,128,16,8,64]{1,4,3,2,0:T(8,128)} %pad_maximum_fusion), calls=%async_computation.1 | async-start | bytes 33554432 | tf_op jit(solution)/shard_map/all_to_all | solution.py:19
